TPU v7x, 256 devices: a whole 4x4x8 slice. The times are simulated.
256 devices in a mesh: layer: 2 (over x_lo), row: 8 (over z), col: 16 (over y, x_hi, core).
Axes of the slice: x: 4 (x_hi: 2, x_lo: 2; x = x_hi * 2 + x_lo), y: 4, z: 8, core: 2. Of those that a mesh axis runs over, the one named last changes fastest.
Arguments:
- left_matrix: float32 [2, 2048, 16384], P(None, 'row', 'col'), may hold values from -6 to 6
- right_matrix: float32 [2, 16384, 2048], P(None, 'row', 'col'), may hold values from -0.03125 to 0.03125
Outputs:
- product: float32 [2, 2048, 2048], P(None, 'row', 'col')
All inputs are finite; a program needn't handle non-finite values.
Results may differ from a plain program's by a relative error of at most 0.000071.
Values sent between devices are 32-bit elements; how exact they have to be, the bound alone decides.
A program may use at most 128 MiB of HBM per device.

v0:
```python
import jax
import jax.numpy as jnp
from jax import lax
from jax.sharding import PartitionSpec as P


def joined_along(pieces, dim):
    pieces = jnp.moveaxis(pieces, 0, dim)
    lengths = pieces.shape
    return pieces.reshape(*lengths[:dim], lengths[dim] * lengths[dim + 1], *lengths[dim + 2 :])


def from_everyone(array, axis):
    size = lax.axis_size(axis)
    return lax.all_to_all(
        jnp.broadcast_to(array[None], (size, *array.shape)), axis, 0, 0, tiled=True
    )


def gather_directly(array, axis, dim):
    return joined_along(from_everyone(array, axis), dim)


def total_of_pieces(array, axis):
    return lax.all_gather(array, axis).sum(0)


def gauss_fold(right_whole, site_rows, cols_out):
    right_real = right_whole[0]
    right_imag = right_whole[1]
    right_total = right_real + right_imag
    highest = lax.Precision.HIGHEST
    empty = jnp.zeros((site_rows, cols_out), jnp.float32)

    def accumulate(totals, segment, offset):
        left_real = segment[0]
        left_imag = segment[1]
        first_term = jnp.dot(
            left_real, right_real, precision=highest, preferred_element_type=jnp.float32
        )
        second_term = jnp.dot(
            left_imag, right_imag, precision=highest, preferred_element_type=jnp.float32
        )
        third_term = jnp.dot(
            left_real + left_imag,
            right_total,
            precision=highest,
            preferred_element_type=jnp.float32,
        )
        return (first_term, second_term, third_term)

    return (accumulate, (empty, empty, empty))


def combine_terms(totals):
    first_term, second_term, third_term = totals
    return jnp.stack([first_term - second_term, third_term - first_term - second_term])


def local(left_matrix, right_matrix):
    layers = lax.axis_size("layer")
    layer_index = lax.axis_index("layer")
    local_rows = left_matrix.shape[1]
    local_cols = right_matrix.shape[2]
    left_width = left_matrix.shape[2]
    right_height = right_matrix.shape[1]
    share_width = left_width // layers
    group_count = right_height // left_width
    left_own = lax.dynamic_slice_in_dim(left_matrix, layer_index * share_width, share_width, 2)
    right_view = right_matrix.reshape(2, group_count, layers, share_width, local_cols)
    right_own = lax.dynamic_slice_in_dim(right_view, layer_index, 1, 2)
    right_own = right_own.reshape(2, group_count * share_width, local_cols)
    right_whole = gather_directly(right_own, "row", 1)
    accumulate, initial = gauss_fold(right_whole, local_rows, local_cols)
    totals = accumulate(initial, lax.all_gather(left_own, "col", axis=2, tiled=True), jnp.int32(0))
    partial_product = combine_terms(totals)
    product = total_of_pieces(partial_product, "layer")
    return product


def solution(mesh):
    in_specs = (P(None, "row", "col"), P(None, "row", "col"))
    out_specs = P(None, "row", "col")
    return jax.shard_map(local, mesh=mesh, in_specs=in_specs, out_specs=out_specs, check_vma=False)
```

profile of v0, /device:TPU:1, one launch (start us, length us, event | category | flops | bytes accessed | tf_op | source)
XLA Modules:
  0.0 248.9 jit_solution(7307586917868702117)
XLA Ops:
  6.5 0.0 copy-start
  6.5 0.0 all-gather.3.cloned.1.call-start
  6.5 2.5 constant_dynamic-slice_fusion.1
  9.0 0.0 all-gather.3.cloned.1.call-update
  9.0 0.0 copy-done
  9.0 0.1 constant_dynamic-slice_fusion
  9.1 0.8 broadcast_in_dim.8
  9.9 193.4 %all_to_all.5 = f32[8,2,1024,128]{3,2,1,0:T(8,128)S(1)} all-to-all(f32[8,2,1024,128]{3,2,1,0:T(8,128)S(1)} %broadcast_in_dim.8), channel_id=1, replica_groups=mesh['layer'=2,'row'=8,'col'=16] {'row'}, dimensions={0} | all-to-all | bytes 16777216 | tf_op jit(solution)/shard_map/all_to_all | solution.py:15
  203.4 5.1 %slice_add_fusion = (f32[1,8,1024,128]{3,2,0,1:T(8,128)}, f32[1,8,1024,128]{3,2,0,1:T(8,128)}, f32[1,8,1024,128]{3,2,0,1:T(8,128)}) fusion(f32[2,8,1024,128]{3,2,0,1:T(8,128)S(1)} %bitcast.30), kind=kLoop, calls=%fused_computation.18 | loop fusion | flops 1048576 | bytes 20971520 | tf_op jit(solution)/shard_map/add | solution.py:31
  208.5 0.0 all-gather.3.cloned.1.call-done
  208.5 0.0 copy-start.1
  208.5 9.9 %fusion.2 = f32[256,128]{1,0:T(8,128)S(1)} fusion(f32[8192,128]{1,0:T(8,128)} %bitcast.33, f32[2,256,8192]{2,1,0:T(8,128)} %all-gather.3.cloned.1.call-done), kind=kOutput, calls=%fused_computation.2 | convolution fusion | flops 3221225472 | bytes 12713984 | tf_op jit(solution)/shard_map/dot_general | solution.py:41
  218.4 0.0 copy-start.2
  218.4 10.1 %fusion.4 = f32[256,128]{1,0:T(8,128)S(1)} fusion(f32[8192,128]{1,0:T(8,128)} %bitcast.32, f32[2,256,8192]{2,1,0:T(8,128)} %all-gather.3.cloned.1.call-done), kind=kOutput, calls=%fused_computation.4 | convolution fusion | flops 3221225472 | bytes 12713984 | tf_op jit(solution)/shard_map/dot_general | solution.py:38
  228.6 0.0 copy-done.1
  228.6 0.0 copy-done.2
  228.6 6.8 %fusion.17 = f32[1,256,128]{2,1,0:T(8,128)S(1)} fusion(f32[256,128]{1,0:T(8,128)S(1)} %fusion.2, f32[256,128]{1,0:T(8,128)S(1)} %fusion.4, f32[8192,128]{1,0:T(8,128)S(1)} %bitcast.31, f32[2,256,8192]{2,1,0:T(8,128)S(1)} %copy-done.1), kind=kOutput, calls=%fused_computation.13 | convolution fusion | flops 3223388160 | bytes 21364736 | tf_op jit(solution)/shard_map/dot_general | solution.py:44
  235.5 5.9 %all-gather = f32[4,256,128]{2,1,0:T(8,128)S(1)} all-gather(f32[2,256,128]{2,1,0:T(8,128)S(1)} %pad_maximum_fusion), channel_id=2, replica_groups=mesh['layer'=2,'row'=8,'col'=16] {'layer'}, dimensions={0}, use_global_device_ids=true | all-gather | bytes 786432 | tf_op jit(solution)/shard_map/all_gather | solution.py:25
  241.3 0.7 reduce_sum.9
  (2 shorter events, 0.0 us)
Async XLA Ops:
  6.5 2.5 %copy-start = (f32[2,2048,128]{2,1,0:T(8,128)S(1)}, f32[2,2048,128]{2,1,0:T(8,128)}, u32[]{:S(2)}) copy-start(f32[2,2048,128]{2,1,0:T(8,128)} %param.3) | copy-start | bytes 6291460
  6.5 202.0 %all-gather.3.cloned.1.call-start = ((), (), s32[]{:S(2)}) async-start(), calls=%async_computation.1 | async-start | bytes 17825792 | tf_op jit(solution)/shard_map/all_gather | solution.py:75
  208.5 20.1 %copy-start.1 = (f32[2,256,8192]{2,1,0:T(8,128)S(1)}, f32[2,256,8192]{2,1,0:T(8,128)}, u32[]{:S(2)}) copy-start(f32[2,256,8192]{2,1,0:T(8,128)} %all-gather.3.cloned.1.call-done) | copy-start | bytes 50331652
  218.4 10.2 %copy-start.2 = (f32[1,8,1024,128]{3,2,0,1:T(8,128)S(1)}, f32[1,8,1024,128]{3,2,0,1:T(8,128)}, u32[]{:S(2)}) copy-start(f32[1,8,1024,128]{3,2,0,1:T(8,128)} %get-tuple-element.5) | copy-start | bytes 12582916
Sparse Core Ops, SparseCore 0:
  10.1 117.9 all-gather.2
where the time goes:
time: 251 us; the launch traced here: 249 us
  blocking collectives  199 us (79%)
  matrix products  26.9 us (11%)
  between operations  13.5 us (5%)
  other arithmetic  5.86 us (2%)
  local copies, waits for them, and re-layouts  3.36 us (1%)
    all_to_all x1, blocking collectives, from_everyone(): lax.all_to_all(jnp.broadcast_to(array[None], (size, *array.shape)), axis,...  193 us
    dot_general x1, matrix products, accumulate(): jnp.dot(left_real, right_real, precision=highest, preferred_element_type=...  10.1 us
    dot_general x1, matrix products, accumulate(): jnp.dot(left_imag, right_imag, precision=highest, preferred_element_type=...  9.93 us
    dot_general x1, matrix products, accumulate(): jnp.dot(left_real + left_imag, right_total, precision=highest, preferred_...  6.81 us
    all_gather x1, blocking collectives, total_of_pieces(): return lax.all_gather(array, axis).sum(0)  5.89 us
    add x1, other arithmetic, gauss_fold(): right_total = right_real + right_imag  5.1 us
  transfers between devices with their start and end apart: 1, of which 0 were waited for; matrix products, arithmetic and copies ran while one was open for 2% of the time, Pallas kernels for 0%

commit v1 on v0

--- a/solution.py
+++ b/solution.py
@@ -2,23 +2,6 @@
 import jax.numpy as jnp
 from jax import lax
 from jax.sharding import PartitionSpec as P
-
-
-def joined_along(pieces, dim):
-    pieces = jnp.moveaxis(pieces, 0, dim)
-    lengths = pieces.shape
-    return pieces.reshape(*lengths[:dim], lengths[dim] * lengths[dim + 1], *lengths[dim + 2 :])
-
-
-def from_everyone(array, axis):
-    size = lax.axis_size(axis)
-    return lax.all_to_all(
-        jnp.broadcast_to(array[None], (size, *array.shape)), axis, 0, 0, tiled=True
-    )
-
-
-def gather_directly(array, axis, dim):
-    return joined_along(from_everyone(array, axis), dim)
 
 
 def total_of_pieces(array, axis):
@@ -29,7 +12,7 @@
     right_real = right_whole[0]
     right_imag = right_whole[1]
     right_total = right_real + right_imag
-    highest = lax.Precision.HIGHEST
+    highest = lax.Precision.HIGH
     empty = jnp.zeros((site_rows, cols_out), jnp.float32)
 
     def accumulate(totals, segment, offset):
@@ -70,7 +53,7 @@
     right_view = right_matrix.reshape(2, group_count, layers, share_width, local_cols)
     right_own = lax.dynamic_slice_in_dim(right_view, layer_index, 1, 2)
     right_own = right_own.reshape(2, group_count * share_width, local_cols)
-    right_whole = gather_directly(right_own, "row", 1)
+    right_whole = lax.all_gather(right_own, "row", axis=1, tiled=True)
     accumulate, initial = gauss_fold(right_whole, local_rows, local_cols)
     totals = accumulate(initial, lax.all_gather(left_own, "col", axis=2, tiled=True), jnp.int32(0))
     partial_product = combine_terms(totals)

time: 251 us -> 263 us (1.048)
  waiting for transfers between devices: 0.02 us -> 211 us
  blocking collectives: 199 us -> 8.27 us
  other arithmetic: 5.86 us -> 0.77 us
  matrix products: 26.9 us -> 23.7 us
    all_to_all x1 -> x0, blocking collectives: 193 us -> none  [from_everyone(): lax.all_to_all(jnp.broadcast_to(array[None], (size, *array.shape)), axis,...]
    all_gather x1, waiting for transfers between devices: 0.01 us -> 116 us  [local(): lax.all_gather(left_own, 'col', axis=2, tiled=True)]
    all_gather x0 -> x1, waiting for transfers between devices: none -> 95.5 us  [local(): right_whole = lax.all_gather(right_own, 'row', axis=1, tiled=True)]
    add x1 -> x0, other arithmetic: 5.1 us -> none  [gauss_fold(): right_total = right_real + right_imag]
    dot_general x1, matrix products: 10.1 us -> 7.11 us  [accumulate(): jnp.dot(left_real, right_real, precision=highest, preferred_element_type=...]
  transfers between devices with their start and end apart: 1 -> 2, of which waited for: 0 -> 2; matrix products, arithmetic and copies ran while one was open for 2% -> 1% of each run, Pallas kernels for 0% -> 0%
where the time goes in v1:
time: 263 us; the launch traced here: 262 us
  waiting for transfers between devices  211 us (80%)
  matrix products  23.7 us (9%)
  between operations  13.5 us (5%)
  blocking collectives  8.27 us (3%)
  local copies, waits for them, and re-layouts  4.96 us (2%)
    all_gather x1, waiting for transfers between devices, local(): lax.all_gather(left_own, 'col', axis=2, tiled=True)  116 us
    all_gather x1, waiting for transfers between devices, local(): right_whole = lax.all_gather(right_own, 'row', axis=1, tiled=True)  95.5 us
    dot_general x1, matrix products, accumulate(): jnp.dot(left_real + left_imag, right_total, precision=highest, preferred_...  8.63 us
    all_gather x1, blocking collectives, total_of_pieces(): return lax.all_gather(array, axis).sum(0)  8.27 us
    dot_general x1, matrix products, accumulate(): jnp.dot(left_imag, right_imag, precision=highest, preferred_element_type=...  7.93 us
    dot_general x1, matrix products, accumulate(): jnp.dot(left_real, right_real, precision=highest, preferred_element_type=...  7.11 us
  transfers between devices with their start and end apart: 2, of which 2 were waited for; matrix products, arithmetic and copies ran while one was open for 1% of the time, Pallas kernels for 0%

profile of v1, /device:TPU:1, one launch (start us, length us, event | category | flops | bytes accessed | tf_op | source)
XLA Modules:
  0.0 262.4 jit_solution(4417337820127016118)
XLA Ops:
  6.5 0.0 copy-start
  6.5 0.0 all-gather.6.cloned.1.call-start
  6.5 1.6 copy-done
  8.1 1.1 constant_dynamic-slice_fusion
  9.2 0.0 all-gather.6.cloned.1.call-update
  9.3 0.0 all-gather.4.cloned.1.call-start
  9.3 2.3 constant_dynamic-slice_fusion.1
  11.6 0.0 all-gather.4.cloned.1.call-update
  11.6 95.5 %all-gather.6.cloned.1.call-done = f32[2,8192,128]{2,1,0:T(8,128)} async-done(((f32[2,1024,128]{2,1,0:T(8,128)}), f32[2,8192,128]{2,1,0:T(8,128)}) %all-gather.6.cloned.1.call-update) | async-done | bytes 8388624 | tf_op jit(solution)/shard_map/all_gather | solution.py:56
  107.1 115.7 %all-gather.4.cloned.1.call-done = f32[2,256,8192]{2,1,0:T(8,128)} async-done(((f32[2,256,512]{2,1,0:T(8,128)}), f32[2,256,8192]{2,1,0:T(8,128)}) %all-gather.4.cloned.1.call-update) | async-done | bytes 16777232 | tf_op jit(solution)/shard_map/all_gather | solution.py:58
  222.8 0.0 copy-start.1
  222.8 7.9 %fusion.2 = f32[256,128]{1,0:T(8,128)S(1)} fusion(f32[2,256,8192]{2,1,0:T(8,128)} %all-gather.4.cloned.1.call-done, f32[2,8192,128]{2,1,0:T(8,128)} %all-gather.6.cloned.1.call-done), kind=kOutput, calls=%fused_computation.2 | convolution fusion | flops 1610612736 | bytes 12713984 | tf_op jit(solution)/shard_map/dot_general | solution.py:24
  230.7 0.0 copy-done.1
  230.8 7.1 %fusion.4 = f32[256,128]{1,0:T(8,128)S(1)} fusion(f32[2,256,8192]{2,1,0:T(8,128)} %all-gather.4.cloned.1.call-done, f32[2,8192,128]{2,1,0:T(8,128)S(1)} %copy-done.1), kind=kOutput, calls=%fused_computation.4 | convolution fusion | flops 1610612736 | bytes 12713984 | tf_op jit(solution)/shard_map/dot_general | solution.py:21
  237.9 8.6 %fusion.29 = f32[1,256,128]{2,1,0:T(8,128)S(1)} fusion(f32[256,128]{1,0:T(8,128)S(1)} %fusion.2, f32[256,128]{1,0:T(8,128)S(1)} %fusion.4, f32[2,8192,128]{2,1,0:T(8,128)S(1)} %copy-done.1, f32[2,256,8192]{2,1,0:T(8,128)} %all-gather.4.cloned.1.call-done), kind=kOutput, calls=%fused_computation.21 | convolution fusion | flops 1613824000 | bytes 25559040 | tf_op jit(solution)/shard_map/dot_general | solution.py:27
  246.6 8.3 %all-gather = f32[4,256,128]{2,1,0:T(8,128)S(1)} all-gather(f32[2,256,128]{2,1,0:T(8,128)S(1)} %pad_maximum_fusion), channel_id=2, replica_groups=mesh['layer'=2,'row'=8,'col'=16] {'layer'}, dimensions={0}, use_global_device_ids=true | all-gather | bytes 786432 | tf_op jit(solution)/shard_map/all_gather | solution.py:8
  254.8 0.7 reduce_sum.9
  (2 shorter events, 0.0 us)
Async XLA Ops:
  6.5 1.6 copy-start
  6.5 100.6 %all-gather.6.cloned.1.call-start = ((), (), s32[]{:S(2)}) async-start(), calls=%async_computation.1 | async-start | bytes 9437184 | tf_op jit(solution)/shard_map/all_gather | solution.py:56
  9.3 213.6 %all-gather.4.cloned.1.call-start = ((), (), s32[]{:S(2)}) async-start(), calls=%async_computation | async-start | bytes 17825792 | tf_op jit(solution)/shard_map/all_gather | solution.py:58
  222.8 7.9 %copy-start.1 = (f32[2,8192,128]{2,1,0:T(8,128)S(1)}, f32[2,8192,128]{2,1,0:T(8,128)}, u32[]{:S(2)}) copy-start(f32[2,8192,128]{2,1,0:T(8,128)} %all-gather.6.cloned.1.call-done) | copy-start | bytes 25165828
Sparse Core Ops, SparseCore 0:
  9.4 97.6 all-gather.5
  109.9 112.8 all-gather.3

commit v2 on v1

v2 whole, which is shorter than its diff:
```python
import functools

import jax
import jax.numpy as jnp
from jax import lax
from jax.experimental import pallas as pl
from jax.experimental.pallas import tpu as pltpu
from jax.sharding import PartitionSpec as P

MESH = pl.DeviceIdType.MESH
GROUPS = 4
NEAR_FIRST = (0, 1, 7, 2, 6, 3, 5, 4)
FAR_FIRST = (4, 3, 5, 2, 6, 1, 7)
CHUNKS = 4


def bulk_wait(ref, sem):
    pltpu.make_async_copy(ref, ref, sem).wait()


def kernel(
    left_ref, right_ref, out_ref,
    s1, ag, braw, bs, asp, cp, cr, fin, outs,
    a1_send, a1_recv, a2_send, ag_recv, a3_send,
    b_send, b_own, b_par, b_oth, b_oc,
    c_send, c_recv, x_send, x_recv,
):
    G = GROUPS
    l = lax.axis_index("layer")
    z = lax.axis_index("row")
    q = lax.axis_index("col")
    c = q % 2
    h = (q // 2) % 2
    y = q // 4
    a = 2 * h + l
    rg = s1.shape[3]
    width = s1.shape[4]
    sub_rows = rg * G
    mine = a * 2 + c
    slot = h * 2 + c

    def col_of(yy, hh, cc):
        return yy * 4 + hh * 2 + cc

    def dev(dl=0, dz=0, dy=0, dh=0, dc=0):
        return ((l + dl) % 2, (z + dz) % 8, col_of((y + dy) % 4, (h + dh) % 2, (c + dc) % 2))

    def send(src, dst, send_sem, recv_sem, device):
        pltpu.make_async_remote_copy(
            src_ref=src, dst_ref=dst, send_sem=send_sem, recv_sem=recv_sem,
            device_id=device, device_id_type=MESH,
        ).start()

    partners = set()
    for dx in (0, 1):
        for dy in range(4):
            for dc in range(2):
                partners.add((dx, 0, dy, dx, dc))
    for dz in range(1, 8):
        partners.add((0, dz, 0, 0, 0))
    for dl in range(2):
        for dh in range(2):
            for dc in range(2):
                partners.add((dl, 0, 0, dh, dc))
    partners.discard((0, 0, 0, 0, 0))
    partners = sorted(partners)
    barrier = pltpu.get_barrier_semaphore()
    for partner in partners:
        pl.semaphore_signal(barrier, inc=1, device_id=dev(*partner), device_id_type=MESH)
    pl.semaphore_wait(barrier, len(partners))

    def scatter(g):
        for dx in (1, 0):
            at = (2 * h + l) if dx == 0 else (2 * (1 - h) + (1 - l))
            for dy in (2, 1, 3, 0):
                for dc in (1, 0):
                    rows = (at * 2 + (c + dc) % 2) * sub_rows + g * rg
                    src = left_ref.at[
                        :,
                        pl.ds(pl.multiple_of(rows, rg), rg),
                        pl.ds(pl.multiple_of(((y + dy) % 4) * width, width), width),
                    ]
                    dst = s1.at[g, q]
                    if (dx, dy, dc) == (0, 0, 0):
                        pltpu.make_async_copy(src, dst, a1_recv.at[g, q // 2]).start()
                    else:
                        send(src, dst, a1_send.at[g], a1_recv.at[g, q // 2], dev(dx, 0, dy, dx, dc))

    def to_planes(g):
        for dz in FAR_FIRST:
            k = (z + dz) % 8
            piece = s1.at[g, pl.ds(2 * k, 2)]
            bulk_wait(piece, a1_recv.at[g, k])
            send(piece, ag.at[g, y, :, :, z], a2_send.at[g], ag_recv.at[g, y, z], dev(0, dz))
        bulk_wait(s1.at[g, pl.ds(2 * z, 2)], a1_recv.at[g, z])
        ag[g, y, :, :, z] = s1[g, pl.ds(2 * z, 2)]

    def along_y(g):
        for dz in NEAR_FIRST:
            r = (z + dz) % 8
            piece = ag.at[g, y, :, :, r]
            if dz:
                bulk_wait(piece, ag_recv.at[g, y, r])
                src = piece
            else:
                src = s1.at[g, pl.ds(2 * z, 2)]
            for dy in (1, 3):
                send(src, piece, a3_send.at[g], ag_recv.at[g, y, r], dev(0, 0, dy))

    def relay(g):
        for i, dz in enumerate(NEAR_FIRST):
            r = (z + dz) % 8
            back, onward = (3, 1) if i % 2 == 0 else (1, 3)
            origin = (y + back) % 4
            piece = ag.at[g, origin, :, :, r]
            bulk_wait(piece, ag_recv.at[g, origin, r])
            send(piece, piece, a3_send.at[g], ag_recv.at[g, origin, r], dev(0, 0, onward))

    def settle(g):
        for i, dz in enumerate(NEAR_FIRST):
            r = (z + dz) % 8
            for dy in (1 if i % 2 == 0 else 3, 2):
                origin = (y + dy) % 4
                bulk_wait(ag.at[g, origin, :, :, r], ag_recv.at[g, origin, r])

    depth = braw.shape[2]
    half = depth // 2
    chunk = half // CHUNKS
    other = (1 - h) * 2 + c
    cross = (1 - h) * 2 + (1 - c)

    def piece_rows(which, i):
        return pl.ds(pl.multiple_of(which * half + i * chunk, chunk), chunk)

    def right_out():
        pltpu.make_async_copy(right_ref, braw.at[slot], b_own).start()
        send(right_ref, braw.at[slot], b_send, b_par, dev(dc=1))
        for i in range(CHUNKS):
            rows = piece_rows(1 - l, i)
            send(right_ref.at[:, rows], braw.at[slot, :, rows], b_send, b_oth.at[1 - l, i], dev(1, 0, 0, 1, 0))

    def right_on():
        for i in range(CHUNKS):
            rows = piece_rows(l, i)
            piece = braw.at[other, :, rows]
            bulk_wait(piece, b_oth.at[l, i])
            send(piece, piece, b_send, b_oth.at[l, i], dev(dl=1))
            send(piece, piece, b_send, b_oc.at[l, i], dev(dc=1))

    def right_over():
        for i in range(CHUNKS):
            rows = piece_rows(1 - l, i)
            piece = braw.at[other, :, rows]
            bulk_wait(piece, b_oth.at[1 - l, i])
            send(piece, piece, b_send, b_oc.at[1 - l, i], dev(dc=1))

    def split(x):
        high = x.astype(jnp.bfloat16)
        return high, (x - high.astype(jnp.float32)).astype(jnp.bfloat16)

    def split_right(which, rows):
        cols = pl.ds(pl.multiple_of(which * 128, 128), 128)
        real = braw[which, 0, rows, :]
        imag = braw[which, 1, rows, :]
        for m, x in enumerate((real, imag, real + imag)):
            high, low = split(x)
            bs[m, 0, rows, cols] = high
            bs[m, 1, rows, cols] = low

    def split_whole(which):
        @pl.loop(0, depth // 128)
        def _(i):
            split_right(which, pl.ds(pl.multiple_of(i * 128, 128), 128))

    lines = 8 * rg

    def multiply(g):
        for t in range(8):
            for_k, from_y = t // 4, t % 4
            real = ag[g, from_y, for_k, 0].reshape(lines, width)
            imag = ag[g, from_y, for_k, 1].reshape(lines, width)
            for m, x in enumerate((real, imag, real + imag)):
                high, low = split(x)
                asp[m, :lines, t * width:(t + 1) * width] = high
                asp[m, lines:, t * width:(t + 1) * width] = low
        terms = []
        for m in range(3):
            both = jnp.dot(asp[m], bs[m, 0], preferred_element_type=jnp.float32)
            rest = jnp.dot(asp[m, :lines], bs[m, 1], preferred_element_type=jnp.float32)
            terms.append(both[:lines] + both[lines:] + rest)
        first, second, third = terms
        cp[g, :, 0] = (first - second).reshape(8, rg, 512)
        cp[g, :, 1] = (third - first - second).reshape(8, rg, 512)

    def hand_back(g):
        for dz in FAR_FIRST:
            r = (z + dz) % 8
            send(cp.at[g, r], cr.at[g, z], c_send.at[g], c_recv.at[g, z], dev(0, dz))

    def add_up(g):
        total = cp[g, z]
        for dz in NEAR_FIRST[1:]:
            k = (z + dz) % 8
            bulk_wait(cr.at[g, k], c_recv.at[g, k])
            total = total + cr[g, k]
        for i in range(4):
            fin[g, i] = total[:, :, i * 128:(i + 1) * 128]
        for dl in (1, 0):
            for dh in (1, 0):
                for dc in (1, 0):
                    target = ((h + dh) % 2) * 2 + (c + dc) % 2
                    if dl or dh or dc:
                        send(fin.at[g, target], outs.at[g, mine], x_send.at[g], x_recv.at[g], dev(dl, 0, 0, dh, dc))
        outs[g, mine] = fin[g, slot]

    def finish(g):
        bulk_wait(outs.at[g, pl.ds(0, 7)], x_recv.at[g])
        for i in range(8):
            out_ref[:, i * sub_rows + g * rg:i * sub_rows + (g + 1) * rg, :] = outs[g, i]

    for g in range(G):
        scatter(g)
    right_out()
    to_planes(0)
    to_planes(1)
    along_y(0)
    to_planes(2)
    along_y(1)
    relay(0)
    to_planes(3)
    along_y(2)
    relay(1)
    bulk_wait(braw.at[slot], b_own)
    split_whole(slot)
    bulk_wait(braw.at[h * 2 + 1 - c], b_par)
    split_whole(h * 2 + 1 - c)
    right_on()
    along_y(3)
    relay(2)
    right_over()
    split_whole(other)
    for i in range(CHUNKS):
        for which in (l, 1 - l):
            bulk_wait(braw.at[cross, :, piece_rows(which, i)], b_oc.at[which, i])
    split_whole(cross)
    settle(0)
    multiply(0)
    hand_back(0)
    settle(1)
    relay(3)
    multiply(1)
    hand_back(1)
    add_up(0)
    settle(2)
    multiply(2)
    hand_back(2)
    add_up(1)
    settle(3)
    multiply(3)
    hand_back(3)
    add_up(2)
    add_up(3)
    for g in range(G):
        finish(g)
    for g in range(G):
        bulk_wait(s1.at[g, pl.ds(0, 15)], a1_send.at[g])
        bulk_wait(s1.at[g, pl.ds(0, 14)], a2_send.at[g])
        bulk_wait(ag.at[g, pl.ds(0, 3)], a3_send.at[g])
        bulk_wait(cr.at[g, pl.ds(0, 7)], c_send.at[g])
        bulk_wait(outs.at[g, pl.ds(0, 7)], x_send.at[g])
    bulk_wait(braw.at[pl.ds(0, 3)], b_send)


def local(left_matrix, right_matrix):
    _, rows, left_width = left_matrix.shape
    _, depth, cols = right_matrix.shape
    G = GROUPS
    rg = rows // 8 // G
    width = left_width // 4
    f32, bf16 = jnp.float32, jnp.bfloat16
    dma = pltpu.SemaphoreType.DMA
    return pl.pallas_call(
        kernel,
        out_shape=jax.ShapeDtypeStruct((2, rows, cols), f32),
        in_specs=[pl.BlockSpec(memory_space=pl.ANY)] * 2,
        out_specs=pl.BlockSpec(memory_space=pltpu.VMEM),
        scratch_shapes=[
            pltpu.VMEM((G, 16, 2, rg, width), f32),
            pltpu.VMEM((G, 4, 2, 2, 8, rg, width), f32),
            pltpu.VMEM((4, 2, depth, cols), f32),
            pltpu.VMEM((3, 2, depth, 4 * cols), bf16),
            pltpu.VMEM((3, 16 * rg, depth), bf16),
            pltpu.VMEM((G, 8, 2, rg, 4 * cols), f32),
            pltpu.VMEM((G, 8, 2, rg, 4 * cols), f32),
            pltpu.VMEM((G, 4, 2, rg, cols), f32),
            pltpu.VMEM((G, 8, 2, rg, cols), f32),
            dma((G,)), dma((G, 8)), dma((G,)), dma((G, 4, 8)), dma((G,)),
            dma, dma, dma, dma((2, CHUNKS)), dma((2, CHUNKS)),
            dma((G,)), dma((G, 8)), dma((G,)), dma((G,)),
        ],
        compiler_params=pltpu.CompilerParams(
            collective_id=0, has_side_effects=True, vmem_limit_bytes=60 * 1024 * 1024
        ),
    )(left_matrix, right_matrix)


def solution(mesh):
    spec = P(None, "row", "col")
    return jax.shard_map(local, mesh=mesh, in_specs=(spec, spec), out_specs=spec, check_vma=False)
```

time: 263 us -> 97.5 us (0.37)
  waiting for transfers between devices: 211 us -> 0 us
  Pallas kernels: 0 us -> 95.7 us
  matrix products: 23.7 us -> 0 us
  between operations: 13.5 us -> 0.01 us
  blocking collectives: 8.27 us -> 0 us
  local copies, waits for them, and re-layouts: 4.96 us -> 1.67 us
    all_gather x2 -> x0, waiting for transfers between devices: 211 us -> none  [the longest x1 116 us: local(): lax.all_gather(left_own, 'col', axis=2, tiled=True)]
    pallas_call x0 -> x1, Pallas kernels: none -> 95.7 us  [local(): pl.pallas_call(kernel, out_shape=jax.ShapeDtypeStruct((2, rows, cols), f3...]
    dot_general x3 -> x0, matrix products: 23.7 us -> none  [the longest x1 8.63 us: accumulate(): jnp.dot(left_real + left_imag, right_total, precision=highest, preferred_...]
    all_gather x1 -> x0, blocking collectives: 8.27 us -> none  [total_of_pieces(): return lax.all_gather(array, axis).sum(0)]
    dynamic_slice x2 -> x0, local copies, waits for them, and re-layouts: 3.36 us -> none  [the longest x1 2.26 us: local(): lax.dynamic_slice_in_dim(left_matrix, layer_index * share_width, share_wi...]
  transfers between devices with their start and end apart: 2 -> 0, of which waited for: 2 -> 0; matrix products, arithmetic and copies ran while one was open for 1% -> 0% of each run, Pallas kernels for 0% -> 0%
where the time goes in v2:
time: 97.5 us; the launch traced here: 97.3 us
  Pallas kernels  95.7 us (98%)
  local copies, waits for them, and re-layouts  1.67 us (2%)
    pallas_call x1, Pallas kernels, local(): pl.pallas_call(kernel, out_shape=jax.ShapeDtypeStruct((2, rows, cols), f3...  95.7 us

profile of v2, /device:TPU:1, one launch (start us, length us, event | category | flops | bytes accessed | tf_op | source)
XLA Modules:
  0.0 97.3 jit_solution(5041660325833457579)
XLA Ops:
  0.0 95.7 %shard_map.28 = f32[2,256,128]{2,1,0:T(8,128)} custom-call(f32[2,256,1024]{2,1,0:T(8,128)} %left_ref.1, f32[2,2048,128]{2,1,0:T(8,128)} %right_ref.1), custom_call_target="tpu_custom_call" | custom-call | tf_op jit(solution)/shard_map/pallas_call | solution.py:282
  95.7 1.7 %copy.4 = f32[2,256,128]{2,1,0:T(8,128)} copy(f32[2,256,128]{2,1,0:T(8,128)} %shard_map.28) | data formatting | bytes 524288

commit v3 on v1

v3 whole, which is shorter than its diff:
```python
import functools

import jax
import jax.numpy as jnp
from jax import lax
from jax.experimental import pallas as pl
from jax.experimental.pallas import tpu as pltpu
from jax.sharding import PartitionSpec as P

MESH = pl.DeviceIdType.MESH
GROUPS = 4
FAR_FIRST = (4, 3, 5, 2, 6, 1, 7)
ARRIVAL = (0, *FAR_FIRST)
ARRIVED = ((0,), (1,), (2, 3), (4, 5), (6, 7))
RELAYED = ((0, 2), (1, 3), (4, 6), (5, 7))
RELAY_OF = {i: j for j, pair in enumerate(RELAYED) for i in pair}
CHUNKS = 16


SCATTER, NEAR, FAR, PARTNER, PLANES, Y, RELAY, ON, OVER, CROSS, SETTLE, SPLIT, MUL, BACK, ADD, FINISH, DRAIN = range(17)
PARTS = (((0, 2), (2, 3), (3, 4)), ((0, 2), (2, 3), (3, 4)), ((0, 2), (2, 4)), ((0, 2), (2, 4)))
ORDER = (
    (SCATTER, 0), (NEAR,), (SCATTER, 1), (SCATTER, 2), (PARTNER,), (FAR, 0), (PLANES, 0), (Y, 0, 0, 1),
    (FAR, 1), (FAR, 2), (PLANES, 1), (Y, 1, 0, 1), (FAR, 3), (FAR, 4), (Y, 0, 1, 2), (PLANES, 2),
    (Y, 2, 0, 1), (FAR, 5), (Y, 0, 2, 3), (ON, 0), (Y, 0, 3, 4), (FAR, 6), (ON, 1), (Y, 0, 4, 5),
    (FAR, 7), (ON, 2), (RELAY, 0, 0, 1), (OVER, 0), (RELAY, 0, 1, 2), (FAR, 8), (ON, 3), (Y, 1, 1, 2),
    (OVER, 1), (FAR, 9), (Y, 1, 2, 3), (ON, 4), (RELAY, 0, 2, 3), (OVER, 2), (Y, 1, 3, 4),
    (RELAY, 0, 3, 4), (FAR, 10), (ON, 5), (Y, 1, 4, 5), (OVER, 3), (SCATTER, 3), (ON, 6), (OVER, 4),
    (RELAY, 1, 0, 1), (CROSS, 0), (ON, 7), (RELAY, 1, 1, 2), (Y, 2, 1, 2), (OVER, 5), (FAR, 11),
    (Y, 2, 2, 3), (ON, 8), (OVER, 6), (Y, 2, 3, 4), (FAR, 12), (ON, 9), (Y, 2, 4, 5), (SETTLE, 0),
    (SPLIT, 0), (MUL, 0, 0, 2), (FAR, 13), (BACK, 0, 0, 2), (ON, 10), (OVER, 7), (RELAY, 1, 2, 4),
    (OVER, 8), (FAR, 14), (OVER, 9), (FAR, 15), (CROSS, 1), (MUL, 0, 2, 3), (PLANES, 3), (BACK, 0, 2, 3),
    (ON, 11), (OVER, 10), (Y, 3, 0, 1), (ON, 12), (ADD, 0, 0, 2), (RELAY, 2, 0, 2), (ON, 13), (OVER, 11),
    (ON, 14), (RELAY, 2, 2, 3), (OVER, 12), (Y, 3, 1, 2), (RELAY, 2, 3, 4), (CROSS, 2), (ON, 15),
    (Y, 3, 2, 3), (OVER, 13), (SETTLE, 1), (SPLIT, 1), (MUL, 1, 0, 2), (BACK, 1, 0, 2), (OVER, 14),
    (Y, 3, 3, 5), (MUL, 1, 2, 3), (BACK, 1, 2, 3), (OVER, 15), (ADD, 0, 2, 3), (SETTLE, 2), (SPLIT, 2),
    (MUL, 2, 0, 2), (BACK, 2, 0, 2), (CROSS, 3), (RELAY, 3, 0, 2), (MUL, 0, 3, 4), (BACK, 0, 3, 4),
    (MUL, 1, 3, 4), (BACK, 1, 3, 4), (RELAY, 3, 2, 4), (MUL, 2, 2, 4), (BACK, 2, 2, 4), (ADD, 1, 0, 2),
    (ADD, 1, 2, 3), (ADD, 2, 0, 2), (SETTLE, 3), (SPLIT, 3), (MUL, 3, 0, 2), (BACK, 3, 0, 2),
    (MUL, 3, 2, 4), (BACK, 3, 2, 4), (ADD, 0, 3, 4), (ADD, 1, 3, 4), (ADD, 2, 2, 4), (ADD, 3, 0, 2),
    (ADD, 3, 2, 4), (FINISH, 0), (FINISH, 1), (FINISH, 2), (FINISH, 3), (DRAIN,),
)


def bulk_wait(ref, sem):
    pltpu.make_async_copy(ref, ref, sem).wait()


def kernel(
    left_ref, right_ref, out_ref,
    lbuf, s1, ag, braw, bs, asp, cp, cr, fin, outs,
    l_own, a1_send, a1_recv, a2_send, z_recv, relay_recv, plain_recv, far_recv, a3_send,
    b_send, b_own, b_par, b_oth, b_oc,
    c_send, c_recv, x_send, x_recv,
):
    G = GROUPS
    l = lax.axis_index("layer")
    z = lax.axis_index("row")
    q = lax.axis_index("col")
    c = q % 2
    h = (q // 2) % 2
    y = q // 4
    a = 2 * h + l
    rg = s1.shape[3]
    width = s1.shape[4]
    sub_rows = rg * G
    mine = a * 2 + c
    slot = h * 2 + c

    def col_of(yy, hh, cc):
        return yy * 4 + hh * 2 + cc

    def dev(dl=0, dz=0, dy=0, dh=0, dc=0):
        return ((l + dl) % 2, (z + dz) % 8, col_of((y + dy) % 4, (h + dh) % 2, (c + dc) % 2))

    def send(src, dst, send_sem, recv_sem, device):
        pltpu.make_async_remote_copy(
            src_ref=src, dst_ref=dst, send_sem=send_sem, recv_sem=recv_sem,
            device_id=device, device_id_type=MESH,
        ).start()

    partners = set()
    for dx in (0, 1):
        for dy in range(4):
            for dc in range(2):
                partners.add((dx, 0, dy, dx, dc))
    for dz in range(1, 8):
        partners.add((0, dz, 0, 0, 0))
    for dl in range(2):
        for dh in range(2):
            for dc in range(2):
                partners.add((dl, 0, 0, dh, dc))
    partners.discard((0, 0, 0, 0, 0))
    partners = sorted(partners)
    def split(x):
        high = x.astype(jnp.bfloat16)
        return high, (x - high.astype(jnp.float32)).astype(jnp.bfloat16)

    def split_right(which, rows, block):
        cols = pl.ds(pl.multiple_of(block * 128, 128), 128)
        real = braw[which, 0, rows, :]
        imag = braw[which, 1, rows, :]
        for m, x in enumerate((real, imag, real + imag)):
            high, low = split(x)
            bs[m, 0, rows, cols] = high
            bs[m, 1, rows, cols] = low

    depth = braw.shape[2]

    def split_whole(which, block):
        @pl.loop(0, depth // 128)
        def _(i):
            split_right(which, pl.ds(pl.multiple_of(i * 128, 128), 128), block)

    with jax.named_scope("entry"):
        pltpu.make_async_copy(left_ref, lbuf, l_own).start()
        pltpu.make_async_copy(right_ref, braw.at[slot], b_own).start()
        barrier = pltpu.get_barrier_semaphore()
        for partner in partners:
            pl.semaphore_signal(barrier, inc=1, device_id=dev(*partner), device_id_type=MESH)
        bulk_wait(lbuf, l_own)
        bulk_wait(braw.at[slot], b_own)
        split_whole(slot, c)
        pl.semaphore_wait(barrier, len(partners))

    def scatter(g):
        for dx in (1, 0):
            near_set = ((q // 2 - z + 6) % 8) // 4
            at = (2 * h + l) if dx == 0 else (2 * (1 - h) + (1 - l))
            for dy in (2, 1, 3, 0):
                for dc in (1, 0):
                    rows = (at * 2 + (c + dc) % 2) * sub_rows + g * rg
                    src_index = (
                        slice(None),
                        pl.ds(pl.multiple_of(rows, rg), rg),
                        pl.ds(pl.multiple_of(((y + dy) % 4) * width, width), width),
                    )
                    src = lbuf.at[src_index]
                    dst = s1.at[g, q]
                    if (dx, dy, dc) == (0, 0, 0):
                        pltpu.make_async_copy(
                            left_ref.at[src_index], dst, a1_recv.at[g, near_set]
                        ).start()
                    else:
                        send(src, dst, a1_send, a1_recv.at[g, near_set], dev(dx, 0, dy, dx, dc))

    def to_planes(g):
        for i, dz in enumerate(FAR_FIRST):
            if i % 4 == 0:
                bulk_wait(s1.at[g, pl.ds(0, 8)], a1_recv.at[g, i // 4])
            k = (z + dz) % 8
            send(
                s1.at[g, pl.ds(2 * k, 2)], ag.at[g, y, :, :, z], a2_send, z_recv.at[g, min(dz, 8 - dz) - 1], dev(0, dz)
            )
        ag[g, y, :, :, z] = s1[g, pl.ds(2 * z, 2)]

    def along_y(g, first, last):
        for j in range(first, last):
            if j:
                dz = ARRIVAL[ARRIVED[j][0]]
                bulk_wait(ag.at[g, y, :, :, pl.ds(0, len(ARRIVED[j]))], z_recv.at[g, min(dz, 8 - dz) - 1])
            for i in ARRIVED[j]:
                r = (z + ARRIVAL[i]) % 8
                piece = ag.at[g, y, :, :, r]
                src = piece if i else s1.at[g, pl.ds(2 * z, 2)]
                for side, dy in enumerate((1, 3)):
                    sem = relay_recv.at[g, RELAY_OF[i]] if i % 2 == side else plain_recv.at[g, side]
                    send(src, piece, a3_send, sem, dev(0, 0, dy))

    def relay(g, first, last):
        for j in range(first, last):
            back, onward = (3, 1) if j % 2 == 0 else (1, 3)
            origin = (y + back) % 4
            bulk_wait(ag.at[g, origin, :, :, pl.ds(0, 2)], relay_recv.at[g, j])
            for i in RELAYED[j]:
                piece = ag.at[g, origin, :, :, (z + ARRIVAL[i]) % 8]
                send(piece, piece, a3_send, far_recv.at[g], dev(0, 0, onward))

    def settle(g):
        for side in range(2):
            bulk_wait(ag.at[g, y, :, :, pl.ds(0, 4)], plain_recv.at[g, side])
        bulk_wait(ag.at[g, y], far_recv.at[g])

    half = depth // 2
    quarter = half // 2
    each = CHUNKS // 2
    chunk = quarter // each

    def rows_of(which, core, i):
        return pl.ds(pl.multiple_of(which * half + core * quarter + (i % each) * chunk, chunk), chunk)

    def quarter_of(which, core):
        return pl.ds(pl.multiple_of(which * half + core * quarter, quarter), quarter)

    def near():
        for which, core in ((1 - l, 1 - c), (1 - l, c), (l, 1 - c), (l, c)):
            piece = braw.at[slot, :, quarter_of(which, core)]
            send(piece, piece, b_send, b_par.at[which, core], dev(dc=1))

    near_other = h * 2 + 1 - c

    seen = []

    def first_quarter():
        if not seen:
            bulk_wait(braw.at[near_other, :, quarter_of(1 - l, c)], b_par.at[1 - l, c])
            seen.append(True)

    def far(i):
        first_quarter()
        piece = braw.at[h * 2 + i // each, :, rows_of(1 - l, c, i)]
        send(piece, piece, b_send, b_oth.at[0, i], dev(1, 0, 0, 1, 0))

    def partner():
        first_quarter()
        for which, core in ((1 - l, 1 - c), (l, c), (l, 1 - c)):
            bulk_wait(braw.at[near_other, :, quarter_of(which, core)], b_par.at[which, core])
        split_whole(near_other, 1 - c)

    def on(i):
        which = (1 - h) * 2 + i // each
        rows = rows_of(l, c, i)
        piece = braw.at[which, :, rows]
        bulk_wait(piece, b_oth.at[0, i])
        send(piece, piece, b_send, b_oth.at[1, i], dev(dl=1))
        send(piece, piece, b_send, b_oc.at[0, i // 4], dev(dc=1))
        split_right(which, rows, 2 + i // each)

    def over(i):
        which = (1 - h) * 2 + i // each
        rows = rows_of(1 - l, c, i)
        piece = braw.at[which, :, rows]
        bulk_wait(piece, b_oth.at[1, i])
        send(piece, piece, b_send, b_oc.at[1, i // 4], dev(dc=1))
        split_right(which, rows, 2 + i // each)

    def cross(i):
        which = (1 - h) * 2 + 4 * i // each
        for k in range(2):
            start = (l if k == 0 else 1 - l) * half + (1 - c) * quarter + (4 * i % each) * chunk
            rows = pl.ds(pl.multiple_of(start, chunk), 4 * chunk)
            bulk_wait(braw.at[which, :, rows], b_oc.at[k, i])
            split_right(which, rows, 2 + 4 * i // each)

    lines = 8 * rg

    def split_left(g):
        for t in range(8):
            for_k, from_y = t // 4, t % 4
            real = ag[g, from_y, for_k, 0].reshape(lines, width)
            imag = ag[g, from_y, for_k, 1].reshape(lines, width)
            for m, x in enumerate((real, imag, real + imag)):
                high, low = split(x)
                asp[g, m, :lines, t * width:(t + 1) * width] = high
                asp[g, m, lines:, t * width:(t + 1) * width] = low

    def multiply(g, lo, hi):
        cols = slice(lo * 128, hi * 128)
        terms = []
        for m in range(3):
            both = jnp.dot(asp[g, m], bs[m, 0, :, cols], preferred_element_type=jnp.float32)
            rest = jnp.dot(asp[g, m, :lines], bs[m, 1, :, cols], preferred_element_type=jnp.float32)
            terms.append(both[:lines] + both[lines:] + rest)
        first, second, third = terms
        for part, x in enumerate((first - second, third - first - second)):
            for b in range(lo, hi):
                cp[g, b, :, part] = x[:, (b - lo) * 128:(b - lo + 1) * 128].reshape(8, rg, 128)

    def hand_back(g, lo, hi):
        blocks = pl.ds(lo, hi - lo)
        for dz in FAR_FIRST:
            r = (z + dz) % 8
            send(cp.at[g, blocks, r], cr.at[g, blocks, z], c_send, c_recv.at[g, lo], dev(0, dz))

    def add_up(g, lo, hi):
        blocks = pl.ds(lo, hi - lo)
        bulk_wait(cr.at[g, blocks, pl.ds(0, 7)], c_recv.at[g, lo])
        total = cp[g, blocks, z]
        for dz in FAR_FIRST:
            total = total + cr[g, blocks, (z + dz) % 8]
        fin[g, lo:hi] = total
        for b in range(lo, hi):
            for dl in (1, 0):
                if b >= 2:
                    target = (l + dl) % 2, z, col_of(y, 1 - h, b - 2)
                    send(fin.at[g, b], outs.at[g, mine], x_send, x_recv.at[g], target)
                else:
                    dc = b
                    if dl or dc:
                        send(
                            fin.at[g, (c + dc) % 2], outs.at[g, mine], x_send, x_recv.at[g],
                            dev(dl, 0, 0, 0, dc),
                        )
        if lo == 0:
            outs[g, mine] = fin[g, c]

    def finish(g):
        bulk_wait(outs.at[g, pl.ds(0, 7)], x_recv.at[g])
        for i in range(8):
            out_ref[:, i * sub_rows + g * rg:i * sub_rows + (g + 1) * rg, :] = outs[g, i]

    def drain():
        bulk_wait(s1.at[:, pl.ds(0, 15)], a1_send)
        bulk_wait(s1.at[:, pl.ds(0, 14)], a2_send)
        bulk_wait(ag.at[:, pl.ds(0, 3)], a3_send)
        bulk_wait(cr.at[:, :, pl.ds(0, 7)], c_send)
        bulk_wait(outs.at[:, pl.ds(0, 7)], x_send)
        bulk_wait(braw.at[pl.ds(0, 3)], b_send)

    calls = (
        scatter, near, far, partner, to_planes, along_y, relay, on, over, cross,
        settle, split_left, multiply, hand_back, add_up, finish, drain,
    )
    for code, *numbers in ORDER:
        with jax.named_scope("_".join([calls[code].__name__, *map(str, numbers)])):
            calls[code](*numbers)


def local(left_matrix, right_matrix):
    _, rows, left_width = left_matrix.shape
    _, depth, cols = right_matrix.shape
    G = GROUPS
    rg = rows // 8 // G
    width = left_width // 4
    f32, bf16 = jnp.float32, jnp.bfloat16
    dma = pltpu.SemaphoreType.DMA
    return pl.pallas_call(
        kernel,
        out_shape=jax.ShapeDtypeStruct((2, rows, cols), f32),
        in_specs=[pl.BlockSpec(memory_space=pl.ANY)] * 2,
        out_specs=pl.BlockSpec(memory_space=pltpu.VMEM),
        scratch_shapes=[
            pltpu.VMEM((2, rows, left_width), f32),
            pltpu.VMEM((G, 16, 2, rg, width), f32),
            pltpu.VMEM((G, 4, 2, 2, 8, rg, width), f32),
            pltpu.VMEM((4, 2, depth, cols), f32),
            pltpu.VMEM((3, 2, depth, 4 * cols), bf16),
            pltpu.VMEM((G, 3, 16 * rg, depth), bf16),
            pltpu.VMEM((G, 4, 8, 2, rg, cols), f32),
            pltpu.VMEM((G, 4, 8, 2, rg, cols), f32),
            pltpu.VMEM((G, 4, 2, rg, cols), f32),
            pltpu.VMEM((G, 8, 2, rg, cols), f32),
            dma, dma, dma((G, 2)), dma, dma((G, 4)), dma((G, 4)), dma((G, 2)), dma((G,)), dma,
            dma, dma, dma((2, 2)), dma((2, CHUNKS)), dma((2, CHUNKS // 4)),
            dma, dma((G, 4)), dma, dma((G,)),
        ],
        compiler_params=pltpu.CompilerParams(
            collective_id=0, has_side_effects=True, vmem_limit_bytes=60 * 1024 * 1024
        ),
    )(left_matrix, right_matrix)


def solution(mesh):
    spec = P(None, "row", "col")
    return jax.shard_map(local, mesh=mesh, in_specs=(spec, spec), out_specs=spec, check_vma=False)
```

time: 263 us -> 78.6 us (0.30)
  waiting for transfers between devices: 211 us -> 0 us
  Pallas kernels: 0 us -> 76.8 us
  matrix products: 23.7 us -> 0 us
  between operations: 13.5 us -> 0.01 us
  blocking collectives: 8.27 us -> 0 us
  local copies, waits for them, and re-layouts: 4.96 us -> 1.67 us
    all_gather x2 -> x0, waiting for transfers between devices: 211 us -> none  [the longest x1 116 us: local(): lax.all_gather(left_own, 'col', axis=2, tiled=True)]
    pallas_call x0 -> x1, Pallas kernels: none -> 76.8 us  [local(): pl.pallas_call(kernel, out_shape=jax.ShapeDtypeStruct((2, rows, cols), f3...]
    dot_general x3 -> x0, matrix products: 23.7 us -> none  [the longest x1 8.63 us: accumulate(): jnp.dot(left_real + left_imag, right_total, precision=highest, preferred_...]
    all_gather x1 -> x0, blocking collectives: 8.27 us -> none  [total_of_pieces(): return lax.all_gather(array, axis).sum(0)]
    dynamic_slice x2 -> x0, local copies, waits for them, and re-layouts: 3.36 us -> none  [the longest x1 2.26 us: local(): lax.dynamic_slice_in_dim(left_matrix, layer_index * share_width, share_wi...]
  transfers between devices with their start and end apart: 2 -> 0, of which waited for: 2 -> 0; matrix products, arithmetic and copies ran while one was open for 1% -> 0% of each run, Pallas kernels for 0% -> 0%
where the time goes in v3:
time: 78.6 us; the launch traced here: 78.5 us
  Pallas kernels  76.8 us (98%)
  local copies, waits for them, and re-layouts  1.67 us (2%)
    pallas_call x1, Pallas kernels, local(): pl.pallas_call(kernel, out_shape=jax.ShapeDtypeStruct((2, rows, cols), f3...  76.8 us
    unnamed x1, local copies, waits for them, and re-layouts  1.67 us

profile of v3, /device:TPU:1, one launch (start us, length us, event | category | flops | bytes accessed | tf_op | source)
XLA Modules:
  0.0 78.5 jit_solution(7650359919193775169)
XLA Ops:
  0.0 76.8 %shard_map.28 = f32[2,256,128]{2,1,0:T(8,128)} custom-call(f32[2,256,1024]{2,1,0:T(8,128)} %left_ref.1, f32[2,2048,128]{2,1,0:T(8,128)} %right_ref.1), custom_call_target="tpu_custom_call" | custom-call | tf_op jit(solution)/shard_map/pallas_call | solution.py:327
  76.9 1.7 %copy.4 = f32[2,256,128]{2,1,0:T(8,128)} copy(f32[2,256,128]{2,1,0:T(8,128)} %shard_map.28) | data formatting | bytes 524288

commit v4 on v3

--- a/solution.py
+++ b/solution.py
@@ -18,27 +18,28 @@
 
 
 SCATTER, NEAR, FAR, PARTNER, PLANES, Y, RELAY, ON, OVER, CROSS, SETTLE, SPLIT, MUL, BACK, ADD, FINISH, DRAIN = range(17)
-PARTS = (((0, 2), (2, 3), (3, 4)), ((0, 2), (2, 3), (3, 4)), ((0, 2), (2, 4)), ((0, 2), (2, 4)))
+PARTS = (((0, 2), (2, 3), (3, 4)), ((0, 2), (2, 3), (3, 4)), ((0, 2), (2, 3), (3, 4)), ((0, 2), (2, 4)))
 ORDER = (
-    (SCATTER, 0), (NEAR,), (SCATTER, 1), (SCATTER, 2), (PARTNER,), (FAR, 0), (PLANES, 0), (Y, 0, 0, 1),
-    (FAR, 1), (FAR, 2), (PLANES, 1), (Y, 1, 0, 1), (FAR, 3), (FAR, 4), (Y, 0, 1, 2), (PLANES, 2),
-    (Y, 2, 0, 1), (FAR, 5), (Y, 0, 2, 3), (ON, 0), (Y, 0, 3, 4), (FAR, 6), (ON, 1), (Y, 0, 4, 5),
-    (FAR, 7), (ON, 2), (RELAY, 0, 0, 1), (OVER, 0), (RELAY, 0, 1, 2), (FAR, 8), (ON, 3), (Y, 1, 1, 2),
-    (OVER, 1), (FAR, 9), (Y, 1, 2, 3), (ON, 4), (RELAY, 0, 2, 3), (OVER, 2), (Y, 1, 3, 4),
-    (RELAY, 0, 3, 4), (FAR, 10), (ON, 5), (Y, 1, 4, 5), (OVER, 3), (SCATTER, 3), (ON, 6), (OVER, 4),
-    (RELAY, 1, 0, 1), (CROSS, 0), (ON, 7), (RELAY, 1, 1, 2), (Y, 2, 1, 2), (OVER, 5), (FAR, 11),
-    (Y, 2, 2, 3), (ON, 8), (OVER, 6), (Y, 2, 3, 4), (FAR, 12), (ON, 9), (Y, 2, 4, 5), (SETTLE, 0),
-    (SPLIT, 0), (MUL, 0, 0, 2), (FAR, 13), (BACK, 0, 0, 2), (ON, 10), (OVER, 7), (RELAY, 1, 2, 4),
-    (OVER, 8), (FAR, 14), (OVER, 9), (FAR, 15), (CROSS, 1), (MUL, 0, 2, 3), (PLANES, 3), (BACK, 0, 2, 3),
-    (ON, 11), (OVER, 10), (Y, 3, 0, 1), (ON, 12), (ADD, 0, 0, 2), (RELAY, 2, 0, 2), (ON, 13), (OVER, 11),
-    (ON, 14), (RELAY, 2, 2, 3), (OVER, 12), (Y, 3, 1, 2), (RELAY, 2, 3, 4), (CROSS, 2), (ON, 15),
-    (Y, 3, 2, 3), (OVER, 13), (SETTLE, 1), (SPLIT, 1), (MUL, 1, 0, 2), (BACK, 1, 0, 2), (OVER, 14),
-    (Y, 3, 3, 5), (MUL, 1, 2, 3), (BACK, 1, 2, 3), (OVER, 15), (ADD, 0, 2, 3), (SETTLE, 2), (SPLIT, 2),
-    (MUL, 2, 0, 2), (BACK, 2, 0, 2), (CROSS, 3), (RELAY, 3, 0, 2), (MUL, 0, 3, 4), (BACK, 0, 3, 4),
-    (MUL, 1, 3, 4), (BACK, 1, 3, 4), (RELAY, 3, 2, 4), (MUL, 2, 2, 4), (BACK, 2, 2, 4), (ADD, 1, 0, 2),
-    (ADD, 1, 2, 3), (ADD, 2, 0, 2), (SETTLE, 3), (SPLIT, 3), (MUL, 3, 0, 2), (BACK, 3, 0, 2),
-    (MUL, 3, 2, 4), (BACK, 3, 2, 4), (ADD, 0, 3, 4), (ADD, 1, 3, 4), (ADD, 2, 2, 4), (ADD, 3, 0, 2),
-    (ADD, 3, 2, 4), (FINISH, 0), (FINISH, 1), (FINISH, 2), (FINISH, 3), (DRAIN,),
+    (SCATTER, 0), (NEAR,), (SCATTER, 1), (FAR, 0), (FAR, 1), (FAR, 2), (SCATTER, 2), (PARTNER,),
+    (PLANES, 0), (Y, 0, 0, 1), (FAR, 3), (FAR, 4), (PLANES, 1), (Y, 1, 0, 1), (ON, 0), (FAR, 5),
+    (SCATTER, 3), (ON, 1), (Y, 0, 1, 3), (ON, 2), (Y, 0, 3, 4), (OVER, 0), (Y, 0, 4, 5), (FAR, 6),
+    (OVER, 1), (FAR, 7), (PLANES, 2), (OVER, 2), (Y, 2, 0, 1), (ON, 3), (RELAY, 0, 0, 1), (FAR, 8),
+    (RELAY, 0, 1, 2), (ON, 4), (FAR, 9), (Y, 1, 1, 3), (ON, 5), (RELAY, 0, 2, 3), (FAR, 10),
+    (RELAY, 0, 3, 4), (OVER, 3), (FAR, 11), (OVER, 4), (Y, 1, 3, 4), (CROSS, 0), (FAR, 12), (PLANES, 3),
+    (OVER, 5), (Y, 1, 4, 5), (ON, 6), (RELAY, 1, 0, 1), (FAR, 13), (RELAY, 1, 1, 2), (ON, 7), (FAR, 14),
+    (SETTLE, 0), (SPLIT, 0), (MUL, 0, 0, 2), (FAR, 15), (BACK, 0, 0, 2), (ON, 8), (OVER, 6),
+    (Y, 2, 1, 3), (RELAY, 1, 2, 3), (ON, 9), (RELAY, 1, 3, 4), (OVER, 7), (ON, 10), (Y, 2, 3, 4),
+    (ON, 11), (CROSS, 1), (MUL, 0, 2, 3), (BACK, 0, 2, 3), (OVER, 8), (Y, 2, 4, 5), (ON, 12),
+    (RELAY, 2, 0, 2), (OVER, 9), (ON, 13), (SETTLE, 1), (SPLIT, 1), (MUL, 1, 0, 2), (BACK, 1, 0, 2),
+    (ON, 14), (OVER, 10), (Y, 3, 0, 2), (MUL, 1, 2, 3), (BACK, 1, 2, 3), (ON, 15), (OVER, 11),
+    (RELAY, 2, 2, 4), (OVER, 12), (Y, 3, 2, 3), (OVER, 13), (CROSS, 2), (Y, 3, 3, 4), (OVER, 14),
+    (Y, 3, 4, 5), (SETTLE, 2), (SPLIT, 2), (MUL, 2, 0, 2), (BACK, 2, 0, 2), (OVER, 15), (RELAY, 3, 0, 2),
+    (MUL, 2, 2, 3), (BACK, 2, 2, 3), (CROSS, 3), (RELAY, 3, 2, 3), (MUL, 0, 3, 4), (BACK, 0, 3, 4),
+    (RELAY, 3, 3, 4), (MUL, 1, 3, 4), (BACK, 1, 3, 4), (MUL, 2, 3, 4), (BACK, 2, 3, 4), (SETTLE, 3),
+    (SPLIT, 3), (MUL, 3, 0, 2), (BACK, 3, 0, 2), (MUL, 3, 2, 4), (BACK, 3, 2, 4), (ADD, 0, 0, 2),
+    (ADD, 0, 2, 3), (ADD, 1, 0, 2), (ADD, 1, 2, 3), (ADD, 2, 0, 2), (ADD, 2, 2, 3), (ADD, 0, 3, 4),
+    (ADD, 1, 3, 4), (ADD, 2, 3, 4), (ADD, 3, 0, 2), (ADD, 3, 2, 4), (FINISH, 0), (FINISH, 1),
+    (FINISH, 2), (FINISH, 3), (DRAIN,),
 )
 
 
@@ -326,7 +327,7 @@
     dma = pltpu.SemaphoreType.DMA
     return pl.pallas_call(
         kernel,
-        out_shape=jax.ShapeDtypeStruct((2, rows, cols), f32),
+        out_shape=pltpu.VMEM((2, rows, cols), f32),
         in_specs=[pl.BlockSpec(memory_space=pl.ANY)] * 2,
         out_specs=pl.BlockSpec(memory_space=pltpu.VMEM),
         scratch_shapes=[

time: 78.6 us -> 75.6 us (0.962)
  Pallas kernels: 76.8 us -> 74.8 us
  local copies, waits for them, and re-layouts: 1.67 us -> 0.71 us
    pallas_call x1, Pallas kernels: 76.8 us -> 74.8 us  [local(): pl.pallas_call(kernel, out_shape=pltpu.VMEM((2, rows, cols), f32), in_spe...]
    unnamed x1, local copies, waits for them, and re-layouts: 1.67 us -> 0.71 us
where the time goes in v4:
time: 75.6 us; the launch traced here: 75.5 us
  Pallas kernels  74.8 us (99%)
    pallas_call x1, Pallas kernels, local(): pl.pallas_call(kernel, out_shape=pltpu.VMEM((2, rows, cols), f32), in_spe...  74.8 us

profile of v4, /device:TPU:1, one launch (start us, length us, event | category | flops | bytes accessed | tf_op | source)
XLA Modules:
  0.0 75.5 jit_solution(12378153430450249220)
XLA Ops:
  0.0 74.8 %shard_map.28 = f32[2,256,128]{2,1,0:T(8,128)S(1)} custom-call(f32[2,256,1024]{2,1,0:T(8,128)} %left_ref.1, f32[2,2048,128]{2,1,0:T(8,128)} %right_ref.1), custom_call_target="tpu_custom_call" | custom-call | tf_op jit(solution)/shard_map/pallas_call | solution.py:328
  74.8 0.7 copy.4

commit v5 on v4

--- a/solution.py
+++ b/solution.py
@@ -13,33 +13,34 @@
 ARRIVAL = (0, *FAR_FIRST)
 ARRIVED = ((0,), (1,), (2, 3), (4, 5), (6, 7))
 RELAYED = ((0, 2), (1, 3), (4, 6), (5, 7))
+SPREAD = (0, 1, 3, 2)
 RELAY_OF = {i: j for j, pair in enumerate(RELAYED) for i in pair}
 CHUNKS = 16
 
 
-SCATTER, NEAR, FAR, PARTNER, PLANES, Y, RELAY, ON, OVER, CROSS, SETTLE, SPLIT, MUL, BACK, ADD, FINISH, DRAIN = range(17)
+SCATTER, NEAR, FAR, PARTNER, PLANES, Y, RELAY, ON, OVER, CROSS, SETTLE, SPLIT, MUL, BACK, ADD, FINISH, DRAIN, PLAIN, EARLY, HEAD = range(20)
 PARTS = (((0, 2), (2, 3), (3, 4)), ((0, 2), (2, 3), (3, 4)), ((0, 2), (2, 3), (3, 4)), ((0, 2), (2, 4)))
 ORDER = (
-    (SCATTER, 0), (NEAR,), (SCATTER, 1), (FAR, 0), (FAR, 1), (FAR, 2), (SCATTER, 2), (PARTNER,),
-    (PLANES, 0), (Y, 0, 0, 1), (FAR, 3), (FAR, 4), (PLANES, 1), (Y, 1, 0, 1), (ON, 0), (FAR, 5),
-    (SCATTER, 3), (ON, 1), (Y, 0, 1, 3), (ON, 2), (Y, 0, 3, 4), (OVER, 0), (Y, 0, 4, 5), (FAR, 6),
-    (OVER, 1), (FAR, 7), (PLANES, 2), (OVER, 2), (Y, 2, 0, 1), (ON, 3), (RELAY, 0, 0, 1), (FAR, 8),
-    (RELAY, 0, 1, 2), (ON, 4), (FAR, 9), (Y, 1, 1, 3), (ON, 5), (RELAY, 0, 2, 3), (FAR, 10),
-    (RELAY, 0, 3, 4), (OVER, 3), (FAR, 11), (OVER, 4), (Y, 1, 3, 4), (CROSS, 0), (FAR, 12), (PLANES, 3),
-    (OVER, 5), (Y, 1, 4, 5), (ON, 6), (RELAY, 1, 0, 1), (FAR, 13), (RELAY, 1, 1, 2), (ON, 7), (FAR, 14),
-    (SETTLE, 0), (SPLIT, 0), (MUL, 0, 0, 2), (FAR, 15), (BACK, 0, 0, 2), (ON, 8), (OVER, 6),
-    (Y, 2, 1, 3), (RELAY, 1, 2, 3), (ON, 9), (RELAY, 1, 3, 4), (OVER, 7), (ON, 10), (Y, 2, 3, 4),
-    (ON, 11), (CROSS, 1), (MUL, 0, 2, 3), (BACK, 0, 2, 3), (OVER, 8), (Y, 2, 4, 5), (ON, 12),
-    (RELAY, 2, 0, 2), (OVER, 9), (ON, 13), (SETTLE, 1), (SPLIT, 1), (MUL, 1, 0, 2), (BACK, 1, 0, 2),
-    (ON, 14), (OVER, 10), (Y, 3, 0, 2), (MUL, 1, 2, 3), (BACK, 1, 2, 3), (ON, 15), (OVER, 11),
-    (RELAY, 2, 2, 4), (OVER, 12), (Y, 3, 2, 3), (OVER, 13), (CROSS, 2), (Y, 3, 3, 4), (OVER, 14),
-    (Y, 3, 4, 5), (SETTLE, 2), (SPLIT, 2), (MUL, 2, 0, 2), (BACK, 2, 0, 2), (OVER, 15), (RELAY, 3, 0, 2),
-    (MUL, 2, 2, 3), (BACK, 2, 2, 3), (CROSS, 3), (RELAY, 3, 2, 3), (MUL, 0, 3, 4), (BACK, 0, 3, 4),
-    (RELAY, 3, 3, 4), (MUL, 1, 3, 4), (BACK, 1, 3, 4), (MUL, 2, 3, 4), (BACK, 2, 3, 4), (SETTLE, 3),
-    (SPLIT, 3), (MUL, 3, 0, 2), (BACK, 3, 0, 2), (MUL, 3, 2, 4), (BACK, 3, 2, 4), (ADD, 0, 0, 2),
-    (ADD, 0, 2, 3), (ADD, 1, 0, 2), (ADD, 1, 2, 3), (ADD, 2, 0, 2), (ADD, 2, 2, 3), (ADD, 0, 3, 4),
-    (ADD, 1, 3, 4), (ADD, 2, 3, 4), (ADD, 3, 0, 2), (ADD, 3, 2, 4), (FINISH, 0), (FINISH, 1),
-    (FINISH, 2), (FINISH, 3), (DRAIN,),
+    (SCATTER, 0), (NEAR,), (SCATTER, 1), (SCATTER, 2), (PARTNER,), (PLANES, 0), (Y, 0, 0, 1), (FAR, 0),
+    (SCATTER, 3), (PLANES, 1), (Y, 1, 0, 1), (FAR, 1), (Y, 0, 1, 2), (PLANES, 2), (Y, 2, 0, 1), (FAR, 2),
+    (Y, 0, 2, 3), (ON, 0), (Y, 0, 3, 4), (FAR, 3), (Y, 0, 4, 5), (PLAIN, 0), (FAR, 4), (PLANES, 3),
+    (OVER, 0), (FAR, 5), (ON, 1), (RELAY, 0, 0, 2), (Y, 1, 1, 2), (FAR, 6), (Y, 1, 2, 3), (ON, 2),
+    (RELAY, 0, 2, 4), (Y, 1, 3, 4), (FAR, 7), (ON, 3), (Y, 1, 4, 5), (OVER, 1), (FAR, 8), (ON, 4),
+    (OVER, 2), (FAR, 9), (PLAIN, 1), (ON, 5), (RELAY, 1, 0, 2), (OVER, 3), (FAR, 10), (ON, 6),
+    (SETTLE, 0), (SPLIT, 0), (OVER, 4), (FAR, 11), (ON, 7), (CROSS, 0), (RELAY, 1, 2, 4), (OVER, 5),
+    (FAR, 12), (ON, 8), (MUL, 0, 0, 2), (FAR, 13), (BACK, 0, 0, 2), (ON, 9), (OVER, 6), (Y, 2, 1, 5),
+    (OVER, 7), (FAR, 14), (ON, 10), (PLAIN, 2), (OVER, 8), (FAR, 15), (ON, 11), (CROSS, 1),
+    (MUL, 0, 2, 3), (BACK, 0, 2, 3), (ON, 12), (OVER, 9), (RELAY, 2, 0, 2), (SETTLE, 1), (SPLIT, 1),
+    (MUL, 1, 0, 2), (BACK, 1, 0, 2), (ON, 13), (OVER, 10), (RELAY, 2, 2, 4), (OVER, 11), (ON, 14),
+    (MUL, 1, 2, 3), (BACK, 1, 2, 3), (OVER, 12), (Y, 3, 0, 1), (ON, 15), (CROSS, 2), (Y, 3, 1, 4),
+    (OVER, 13), (Y, 3, 4, 5), (PLAIN, 3), (OVER, 14), (SETTLE, 2), (SPLIT, 2), (MUL, 2, 0, 2),
+    (BACK, 2, 0, 2), (OVER, 15), (RELAY, 3, 0, 2), (MUL, 2, 2, 3), (BACK, 2, 2, 3), (RELAY, 3, 2, 4),
+    (CROSS, 3), (MUL, 0, 3, 4), (BACK, 0, 3, 4), (MUL, 1, 3, 4), (BACK, 1, 3, 4), (EARLY, 3),
+    (MUL, 2, 3, 4), (BACK, 2, 3, 4), (HEAD, 3, 2, 4), (HEAD, 3, 0, 2), (SETTLE, 3), (SPLIT, 3),
+    (MUL, 3, 2, 4), (BACK, 3, 2, 4), (MUL, 3, 0, 2), (BACK, 3, 0, 2), (ADD, 0, 0, 2), (ADD, 0, 2, 3),
+    (ADD, 1, 0, 2), (ADD, 1, 2, 3), (ADD, 2, 0, 2), (ADD, 2, 2, 3), (ADD, 0, 3, 4), (ADD, 1, 3, 4),
+    (ADD, 2, 3, 4), (ADD, 3, 2, 4), (ADD, 3, 0, 2), (FINISH, 0), (FINISH, 1), (FINISH, 2), (FINISH, 3),
+    (DRAIN,),
 )
 
 
@@ -49,7 +50,7 @@
 
 def kernel(
     left_ref, right_ref, out_ref,
-    lbuf, s1, ag, braw, bs, asp, cp, cr, fin, outs,
+    lbuf, s1, ag, braw, bs, asp, cp, cr, fin, outs, head,
     l_own, a1_send, a1_recv, a2_send, z_recv, relay_recv, plain_recv, far_recv, a3_send,
     b_send, b_own, b_par, b_oth, b_oc,
     c_send, c_recv, x_send, x_recv,
@@ -97,21 +98,26 @@
         high = x.astype(jnp.bfloat16)
         return high, (x - high.astype(jnp.float32)).astype(jnp.bfloat16)
 
-    def split_right(which, rows, block):
+    def split_right(which, start, size, block):
+        rows = pl.ds(pl.multiple_of(start, size), size)
+        tile = start // 256
+        away = (tile % 4 - y + 4) % 4
+        place = away + away // 2 - 2 * (away // 3)
+        into = pl.ds(pl.multiple_of((place * 2 + tile // 4) * 256 + start % 256, size), size)
         cols = pl.ds(pl.multiple_of(block * 128, 128), 128)
         real = braw[which, 0, rows, :]
         imag = braw[which, 1, rows, :]
         for m, x in enumerate((real, imag, real + imag)):
             high, low = split(x)
-            bs[m, 0, rows, cols] = high
-            bs[m, 1, rows, cols] = low
+            bs[m, 0, into, cols] = high
+            bs[m, 1, into, cols] = low
 
     depth = braw.shape[2]
 
     def split_whole(which, block):
         @pl.loop(0, depth // 128)
         def _(i):
-            split_right(which, pl.ds(pl.multiple_of(i * 128, 128), 128), block)
+            split_right(which, i * 128, 128, block)
 
     with jax.named_scope("entry"):
         pltpu.make_async_copy(left_ref, lbuf, l_own).start()
@@ -164,9 +170,14 @@
                 r = (z + ARRIVAL[i]) % 8
                 piece = ag.at[g, y, :, :, r]
                 src = piece if i else s1.at[g, pl.ds(2 * z, 2)]
-                for side, dy in enumerate((1, 3)):
-                    sem = relay_recv.at[g, RELAY_OF[i]] if i % 2 == side else plain_recv.at[g, side]
-                    send(src, piece, a3_send, sem, dev(0, 0, dy))
+                send(src, piece, a3_send, relay_recv.at[g, RELAY_OF[i]], dev(0, 0, 1 if i % 2 == 0 else 3))
+
+    def plain(g):
+        for i in range(8):
+            piece = ag.at[g, y, :, :, (z + ARRIVAL[i]) % 8]
+            src = piece if i else s1.at[g, pl.ds(2 * z, 2)]
+            side = (i + 1) % 2
+            send(src, piece, a3_send, plain_recv.at[g, side], dev(0, 0, (1, 3)[side]))
 
     def relay(g, first, last):
         for j in range(first, last):
@@ -177,9 +188,13 @@
                 piece = ag.at[g, origin, :, :, (z + ARRIVAL[i]) % 8]
                 send(piece, piece, a3_send, far_recv.at[g], dev(0, 0, onward))
 
-    def settle(g):
+    def near_in(g):
         for side in range(2):
             bulk_wait(ag.at[g, y, :, :, pl.ds(0, 4)], plain_recv.at[g, side])
+
+    def settle(g):
+        if g < G - 1:
+            near_in(g)
         bulk_wait(ag.at[g, y], far_recv.at[g])
 
     half = depth // 2
@@ -187,8 +202,11 @@
     each = CHUNKS // 2
     chunk = quarter // each
 
+    def start_of(which, core, i):
+        return which * half + core * quarter + (i % each) * chunk
+
     def rows_of(which, core, i):
-        return pl.ds(pl.multiple_of(which * half + core * quarter + (i % each) * chunk, chunk), chunk)
+        return pl.ds(pl.multiple_of(start_of(which, core, i), chunk), chunk)
 
     def quarter_of(which, core):
         return pl.ds(pl.multiple_of(which * half + core * quarter, quarter), quarter)
@@ -225,7 +243,7 @@
         bulk_wait(piece, b_oth.at[0, i])
         send(piece, piece, b_send, b_oth.at[1, i], dev(dl=1))
         send(piece, piece, b_send, b_oc.at[0, i // 4], dev(dc=1))
-        split_right(which, rows, 2 + i // each)
+        split_right(which, start_of(l, c, i), chunk, 2 + i // each)
 
     def over(i):
         which = (1 - h) * 2 + i // each
@@ -233,7 +251,7 @@
         piece = braw.at[which, :, rows]
         bulk_wait(piece, b_oth.at[1, i])
         send(piece, piece, b_send, b_oc.at[1, i // 4], dev(dc=1))
-        split_right(which, rows, 2 + i // each)
+        split_right(which, start_of(1 - l, c, i), chunk, 2 + i // each)
 
     def cross(i):
         which = (1 - h) * 2 + 4 * i // each
@@ -241,13 +259,13 @@
             start = (l if k == 0 else 1 - l) * half + (1 - c) * quarter + (4 * i % each) * chunk
             rows = pl.ds(pl.multiple_of(start, chunk), 4 * chunk)
             bulk_wait(braw.at[which, :, rows], b_oc.at[k, i])
-            split_right(which, rows, 2 + 4 * i // each)
+            split_right(which, start, 4 * chunk, 2 + 4 * i // each)
 
     lines = 8 * rg
 
-    def split_left(g):
-        for t in range(8):
-            for_k, from_y = t // 4, t % 4
+    def split_tiles(g, first, last):
+        for t in range(first, last):
+            for_k, from_y = t % 2, (y + SPREAD[t // 2]) % 4
             real = ag[g, from_y, for_k, 0].reshape(lines, width)
             imag = ag[g, from_y, for_k, 1].reshape(lines, width)
             for m, x in enumerate((real, imag, real + imag)):
@@ -255,14 +273,28 @@
                 asp[g, m, :lines, t * width:(t + 1) * width] = high
                 asp[g, m, lines:, t * width:(t + 1) * width] = low
 
+    def split_left(g):
+        split_tiles(g, 0 if g < G - 1 else 6, 8)
+
+    def early(g):
+        near_in(g)
+        split_tiles(g, 0, 6)
+
+    def dots(g, m, lo, hi, first, last):
+        deep, cols = slice(first * width, last * width), slice(lo * 128, hi * 128)
+        both = jnp.dot(asp[g, m, :, deep], bs[m, 0, deep, cols], preferred_element_type=jnp.float32)
+        rest = jnp.dot(asp[g, m, :lines, deep], bs[m, 1, deep, cols], preferred_element_type=jnp.float32)
+        return both[:lines] + both[lines:] + rest
+
+    def begin(g, lo, hi):
+        for m in range(3):
+            head[m, :, lo * 128:hi * 128] = dots(g, m, lo, hi, 0, 6)
+
     def multiply(g, lo, hi):
-        cols = slice(lo * 128, hi * 128)
-        terms = []
-        for m in range(3):
-            both = jnp.dot(asp[g, m], bs[m, 0, :, cols], preferred_element_type=jnp.float32)
-            rest = jnp.dot(asp[g, m, :lines], bs[m, 1, :, cols], preferred_element_type=jnp.float32)
-            terms.append(both[:lines] + both[lines:] + rest)
-        first, second, third = terms
+        if g < G - 1:
+            first, second, third = (dots(g, m, lo, hi, 0, 8) for m in range(3))
+        else:
+            first, second, third = (head[m, :, lo * 128:hi * 128] + dots(g, m, lo, hi, 6, 8) for m in range(3))
         for part, x in enumerate((first - second, third - first - second)):
             for b in range(lo, hi):
                 cp[g, b, :, part] = x[:, (b - lo) * 128:(b - lo + 1) * 128].reshape(8, rg, 128)
@@ -310,7 +342,7 @@
 
     calls = (
         scatter, near, far, partner, to_planes, along_y, relay, on, over, cross,
-        settle, split_left, multiply, hand_back, add_up, finish, drain,
+        settle, split_left, multiply, hand_back, add_up, finish, drain, plain, early, begin,
     )
     for code, *numbers in ORDER:
         with jax.named_scope("_".join([calls[code].__name__, *map(str, numbers)])):
@@ -341,6 +373,7 @@
             pltpu.VMEM((G, 4, 8, 2, rg, cols), f32),
             pltpu.VMEM((G, 4, 2, rg, cols), f32),
             pltpu.VMEM((G, 8, 2, rg, cols), f32),
+            pltpu.VMEM((3, 8 * rg, 4 * cols), f32),
             dma, dma, dma((G, 2)), dma, dma((G, 4)), dma((G, 4)), dma((G, 2)), dma((G,)), dma,
             dma, dma, dma((2, 2)), dma((2, CHUNKS)), dma((2, CHUNKS // 4)),
             dma, dma((G, 4)), dma, dma((G,)),

time: 75.6 us -> 72 us (0.952)
  Pallas kernels: 74.8 us -> 71.2 us
    pallas_call x1, Pallas kernels: 74.8 us -> 71.2 us  [local(): pl.pallas_call(kernel, out_shape=pltpu.VMEM((2, rows, cols), f32), in_spe...]
where the time goes in v5:
time: 72 us; the launch traced here: 71.9 us
  Pallas kernels  71.2 us (99%)
    pallas_call x1, Pallas kernels, local(): pl.pallas_call(kernel, out_shape=pltpu.VMEM((2, rows, cols), f32), in_spe...  71.2 us

profile of v5, /device:TPU:1, one launch (start us, length us, event | category | flops | bytes accessed | tf_op | source)
XLA Modules:
  0.0 71.9 jit_solution(10903271021537330326)
XLA Ops:
  0.0 71.2 %shard_map.28 = f32[2,256,128]{2,1,0:T(8,128)S(1)} custom-call(f32[2,256,1024]{2,1,0:T(8,128)} %left_ref.1, f32[2,2048,128]{2,1,0:T(8,128)} %right_ref.1), custom_call_target="tpu_custom_call" | custom-call | tf_op jit(solution)/shard_map/pallas_call | solution.py:360
  71.2 0.7 copy.4

commit v6 on v5

--- a/solution.py
+++ b/solution.py
@@ -125,10 +125,8 @@
         barrier = pltpu.get_barrier_semaphore()
         for partner in partners:
             pl.semaphore_signal(barrier, inc=1, device_id=dev(*partner), device_id_type=MESH)
+        pl.semaphore_wait(barrier, len(partners))
         bulk_wait(lbuf, l_own)
-        bulk_wait(braw.at[slot], b_own)
-        split_whole(slot, c)
-        pl.semaphore_wait(barrier, len(partners))
 
     def scatter(g):
         for dx in (1, 0):
@@ -212,6 +210,7 @@
         return pl.ds(pl.multiple_of(which * half + core * quarter, quarter), quarter)
 
     def near():
+        bulk_wait(braw.at[slot], b_own)
         for which, core in ((1 - l, 1 - c), (1 - l, c), (l, 1 - c), (l, c)):
             piece = braw.at[slot, :, quarter_of(which, core)]
             send(piece, piece, b_send, b_par.at[which, core], dev(dc=1))
@@ -231,6 +230,7 @@
         send(piece, piece, b_send, b_oth.at[0, i], dev(1, 0, 0, 1, 0))
 
     def partner():
+        split_whole(slot, c)
         first_quarter()
         for which, core in ((1 - l, 1 - c), (l, c), (l, 1 - c)):
             bulk_wait(braw.at[near_other, :, quarter_of(which, core)], b_par.at[which, core])

time: 72 us -> 71.9 us (level)
  no operation moved by 1% of the time
where the time goes in v6:
time: 71.9 us; the launch traced here: 71.8 us
  Pallas kernels  71.1 us (99%)
    pallas_call x1, Pallas kernels, local(): pl.pallas_call(kernel, out_shape=pltpu.VMEM((2, rows, cols), f32), in_spe...  71.1 us

profile of v6, /device:TPU:1, one launch (start us, length us, event | category | flops | bytes accessed | tf_op | source)
XLA Modules:
  0.0 71.8 jit_solution(17624239016563353396)
XLA Ops:
  0.0 71.1 %shard_map.28 = f32[2,256,128]{2,1,0:T(8,128)S(1)} custom-call(f32[2,256,1024]{2,1,0:T(8,128)} %left_ref.1, f32[2,2048,128]{2,1,0:T(8,128)} %right_ref.1), custom_call_target="tpu_custom_call" | custom-call | tf_op jit(solution)/shard_map/pallas_call | solution.py:360
  71.1 0.7 copy.4

commit v7 on v6

--- a/solution.py
+++ b/solution.py
@@ -27,20 +27,20 @@
     (OVER, 0), (FAR, 5), (ON, 1), (RELAY, 0, 0, 2), (Y, 1, 1, 2), (FAR, 6), (Y, 1, 2, 3), (ON, 2),
     (RELAY, 0, 2, 4), (Y, 1, 3, 4), (FAR, 7), (ON, 3), (Y, 1, 4, 5), (OVER, 1), (FAR, 8), (ON, 4),
     (OVER, 2), (FAR, 9), (PLAIN, 1), (ON, 5), (RELAY, 1, 0, 2), (OVER, 3), (FAR, 10), (ON, 6),
-    (SETTLE, 0), (SPLIT, 0), (OVER, 4), (FAR, 11), (ON, 7), (CROSS, 0), (RELAY, 1, 2, 4), (OVER, 5),
-    (FAR, 12), (ON, 8), (MUL, 0, 0, 2), (FAR, 13), (BACK, 0, 0, 2), (ON, 9), (OVER, 6), (Y, 2, 1, 5),
-    (OVER, 7), (FAR, 14), (ON, 10), (PLAIN, 2), (OVER, 8), (FAR, 15), (ON, 11), (CROSS, 1),
-    (MUL, 0, 2, 3), (BACK, 0, 2, 3), (ON, 12), (OVER, 9), (RELAY, 2, 0, 2), (SETTLE, 1), (SPLIT, 1),
-    (MUL, 1, 0, 2), (BACK, 1, 0, 2), (ON, 13), (OVER, 10), (RELAY, 2, 2, 4), (OVER, 11), (ON, 14),
-    (MUL, 1, 2, 3), (BACK, 1, 2, 3), (OVER, 12), (Y, 3, 0, 1), (ON, 15), (CROSS, 2), (Y, 3, 1, 4),
-    (OVER, 13), (Y, 3, 4, 5), (PLAIN, 3), (OVER, 14), (SETTLE, 2), (SPLIT, 2), (MUL, 2, 0, 2),
-    (BACK, 2, 0, 2), (OVER, 15), (RELAY, 3, 0, 2), (MUL, 2, 2, 3), (BACK, 2, 2, 3), (RELAY, 3, 2, 4),
-    (CROSS, 3), (MUL, 0, 3, 4), (BACK, 0, 3, 4), (MUL, 1, 3, 4), (BACK, 1, 3, 4), (EARLY, 3),
-    (MUL, 2, 3, 4), (BACK, 2, 3, 4), (HEAD, 3, 2, 4), (HEAD, 3, 0, 2), (SETTLE, 3), (SPLIT, 3),
-    (MUL, 3, 2, 4), (BACK, 3, 2, 4), (MUL, 3, 0, 2), (BACK, 3, 0, 2), (ADD, 0, 0, 2), (ADD, 0, 2, 3),
-    (ADD, 1, 0, 2), (ADD, 1, 2, 3), (ADD, 2, 0, 2), (ADD, 2, 2, 3), (ADD, 0, 3, 4), (ADD, 1, 3, 4),
-    (ADD, 2, 3, 4), (ADD, 3, 2, 4), (ADD, 3, 0, 2), (FINISH, 0), (FINISH, 1), (FINISH, 2), (FINISH, 3),
-    (DRAIN,),
+    (SETTLE, 0), (SPLIT, 0), (OVER, 4), (FAR, 11), (ON, 7), (MUL, 0, 0, 2), (FAR, 12), (BACK, 0, 0, 2),
+    (ON, 8), (OVER, 5), (RELAY, 1, 2, 4), (CROSS, 0), (Y, 2, 1, 3), (OVER, 6), (FAR, 13), (ON, 9),
+    (Y, 2, 3, 5), (OVER, 7), (FAR, 14), (ON, 10), (PLAIN, 2), (OVER, 8), (FAR, 15), (ON, 11),
+    (SETTLE, 1), (CROSS, 1), (OVER, 9), (SPLIT, 1), (ON, 12), (RELAY, 2, 0, 2), (MUL, 0, 2, 3),
+    (BACK, 0, 2, 3), (OVER, 10), (ON, 13), (RELAY, 2, 2, 4), (MUL, 1, 0, 2), (BACK, 1, 0, 2), (ON, 14),
+    (OVER, 11), (MUL, 1, 2, 3), (BACK, 1, 2, 3), (OVER, 12), (Y, 3, 0, 1), (ON, 15), (Y, 3, 1, 3),
+    (OVER, 13), (Y, 3, 3, 4), (CROSS, 2), (Y, 3, 4, 5), (PLAIN, 3), (OVER, 14), (SETTLE, 2), (SPLIT, 2),
+    (MUL, 2, 0, 2), (BACK, 2, 0, 2), (OVER, 15), (RELAY, 3, 0, 2), (MUL, 2, 2, 3), (BACK, 2, 2, 3),
+    (RELAY, 3, 2, 4), (CROSS, 3), (MUL, 0, 3, 4), (BACK, 0, 3, 4), (MUL, 1, 3, 4), (BACK, 1, 3, 4),
+    (EARLY, 3), (MUL, 2, 3, 4), (BACK, 2, 3, 4), (HEAD, 3, 2, 4), (SETTLE, 3), (SPLIT, 3),
+    (MUL, 3, 2, 4), (BACK, 3, 2, 4), (HEAD, 3, 0, 2), (MUL, 3, 0, 2), (BACK, 3, 0, 2), (ADD, 0, 0, 2),
+    (ADD, 0, 2, 3), (ADD, 1, 0, 2), (ADD, 1, 2, 3), (ADD, 2, 0, 2), (ADD, 2, 2, 3), (ADD, 0, 3, 4),
+    (ADD, 1, 3, 4), (ADD, 2, 3, 4), (ADD, 3, 2, 4), (ADD, 3, 0, 2), (FINISH, 0), (FINISH, 1),
+    (FINISH, 2), (FINISH, 3), (DRAIN,),
 )
 
 

time: 71.9 us -> 72.1 us (level)
  no operation moved by 1% of the time
where the time goes in v7:
time: 72.1 us; the launch traced here: 72 us
  Pallas kernels  71.3 us (99%)
    pallas_call x1, Pallas kernels, local(): pl.pallas_call(kernel, out_shape=pltpu.VMEM((2, rows, cols), f32), in_spe...  71.3 us

profile of v7, /device:TPU:1, one launch (start us, length us, event | category | flops | bytes accessed | tf_op | source)
XLA Modules:
  0.0 72.0 jit_solution(12967694869396704577)
XLA Ops:
  0.0 71.3 %shard_map.28 = f32[2,256,128]{2,1,0:T(8,128)S(1)} custom-call(f32[2,256,1024]{2,1,0:T(8,128)} %left_ref.1, f32[2,2048,128]{2,1,0:T(8,128)} %right_ref.1), custom_call_target="tpu_custom_call" | custom-call | tf_op jit(solution)/shard_map/pallas_call | solution.py:360
  71.3 0.7 copy.4
